TPU v7x, 512 devices: a 8x2x16 block of a 8x8x16 slice. The times are simulated.
512 devices in a mesh: groups: 2 (over y), wide: 128 (over x, z), narrow: 2 (over core).
Axes of the slice: x: 8, y: 2, z: 16, core: 2. Of those that a mesh axis runs over, the one named last changes fastest.
The devices are a block of a 8x8x16 slice.
Arguments:
- hidden_in: bfloat16 [102400, 1024], P(('groups', 'wide')), parts along dimension 0, may hold values from -6 to 6
- ffn_gain: bfloat16 [1024], replicated, may hold values from 0.5 to 1.5
- wi_gate: bfloat16 [1024, 2816], P('wide', 'narrow'), may hold values from -0.1875 to 0.1875
- wi_up: bfloat16 [1024, 2816], P('wide', 'narrow'), may hold values from -0.1875 to 0.1875
- wo_down: bfloat16 [2816, 1024], P('narrow', 'wide'), may hold values from -0.109375 to 0.109375
- final_gain: bfloat16 [1024], replicated, may hold values from 0.5 to 1.5
- key_w: bfloat16 [1024, 1024], P('wide', 'narrow'), may hold values from -0.1875 to 0.1875
- value_w: bfloat16 [1024, 1024], P('wide', 'narrow'), may hold values from -0.1875 to 0.1875
- query_w: bfloat16 [1024, 1024], P('wide', 'narrow'), may hold values from -8 to 8
- out_w: bfloat16 [1024, 1024], P('narrow', 'wide'), may hold values from -0.1875 to 0.1875
- dec_gain: bfloat16 [1024], replicated, may hold values from 0.5 to 1.5
- embed: bfloat16 [32128, 1024], P('wide'), may hold values from -6 to 6
- lengths: int32 [512], P(('groups', 'wide')), parts along dimension 0, may hold values from 40 to 200
- answer_ids: int32 [8, 32], P('groups'), parts along dimension 0, may hold values from 0 to 32127
Outputs:
- memory: bfloat16 [102400, 1024], P(('groups', 'wide')), parts along dimension 0
- decoded: bfloat16 [256, 1024], P('groups', 'narrow'), parts along dimension 0
There are 2 independent parts, one for each index of `groups`. A program takes and returns all parts, laid end to end along the dimension named above; an argument that names none is the same for every part. Nothing has to cross between parts.
All inputs are finite; a program needn't handle non-finite values.
Results may differ from a plain program's by a relative error of at most 0.0095.
The roundings to bfloat16 on the way count: a program that leaves them out, or rounds other values in their place, can miss the bound.
Values may be sent and summed in bfloat16 or wider, within the bound.
A program may use at most 64 MiB of HBM per device.

v0:
```python
import math
import jax
import jax.numpy as jnp
from jax import lax
from jax.sharding import Mesh
from jax.sharding import PartitionSpec as P

HEAD_DIM = 64
QUEST = 4
WIDE = ("wide_0", "wide_1")
GROUPS_WIDE = ("groups", "wide_0", "wide_1")
EPS = 1e-06
FLOOR = -1e30


def in_one_piece(arrays, axis, dim, along):
    ends, at = ([], 0)
    for a in arrays[:-1]:
        at += a.shape[along]
        ends.append(at)
    both = jnp.concatenate(arrays, axis=along)
    return tuple(jnp.split(lax.all_gather(both, axis, axis=dim, tiled=True), ends, axis=along))


def in_order(tiles, dim):
    tiles = jnp.moveaxis(tiles, 0, dim)
    lengths = tiles.shape
    return tiles.reshape(*lengths[:dim], lengths[dim] * lengths[dim + 1], *lengths[dim + 2 :])


def all_blocks(x, axes, turns):
    tiles = x
    for k in turns:
        tiles = lax.all_gather(tiles, axes[k])
    done = turns[::-1]
    back = [done.index(k) for k in range(len(axes))]
    tiles = tiles.transpose(*back, *range(len(axes), tiles.ndim))
    return tiles.reshape(-1, *x.shape)


def whole_of(x, axes, turns, dim):
    return in_order(all_blocks(x, axes, turns), dim)


def from_everyone(x, axis):
    copies = jnp.broadcast_to(x, (lax.axis_size(axis), *x.shape))
    return lax.all_to_all(copies, axis, split_axis=0, concat_axis=0, tiled=True)


def over_copies(x, axis):
    return from_everyone(x, axis).sum(axis=0)


def collected_together(x, axis):
    leaves = jax.tree.leaves(x)
    turns = sorted(range(len(leaves)), key=lambda k: -leaves[k].size)
    width = (1, *leaves[turns[0]].shape)[-1]
    lines = [
        jnp.pad(leaves[k].reshape(-1), (0, -leaves[k].size % width)).reshape(-1, width)
        for k in turns
    ]
    both, at, found = (lax.all_gather(jnp.concatenate(lines), axis), 0, {})
    for k, line in zip(turns, lines):
        piece = both[:, at : at + len(line)].reshape(len(both), -1)
        found[k] = piece[:, : leaves[k].size].reshape(-1, *leaves[k].shape)
        at += len(line)
    numbers = iter(range(len(leaves)))
    return jax.tree.map(lambda _: found[next(numbers)], x)


def joined_all(x, axes, combine):
    for axis in axes:
        pieces = collected_together(x, axis)
        x = jax.tree.map(lambda part: part[0], pieces)
        for k in range(1, lax.axis_size(axis)):
            x = combine(x, jax.tree.map(lambda part: part[k], pieces))
    return x


def split_up(x, dim, devices):
    lengths = x.shape
    tiles = x.reshape(*lengths[:dim], devices, lengths[dim] // devices, *lengths[dim + 1 :])
    return jnp.moveaxis(tiles, dim, 0)


def sum_at_owner(x, axis, dim):
    tiles = split_up(x, dim, lax.axis_size(axis))
    arrived = lax.all_to_all(tiles, axis, split_axis=0, concat_axis=0, tiled=True)
    return arrived.astype(jnp.float32).sum(axis=0)


def rms_scale(values, gain):
    mean_square = jnp.mean(values * values, axis=-1, keepdims=True)
    return values * lax.rsqrt(mean_square + EPS) * gain.astype(jnp.float32)


def join_partial(first, second):
    top_first, total_first, acc_first = first
    top_second, total_second, acc_second = second
    top = jnp.maximum(top_first, top_second)
    factor_first = jnp.exp(top_first - top)
    factor_second = jnp.exp(top_second - top)
    width = acc_first.shape[1] // top.shape[1]
    total = total_first * factor_first + total_second * factor_second
    acc = acc_first * jnp.repeat(factor_first, width, axis=1) + acc_second * jnp.repeat(
        factor_second, width, axis=1
    )
    return (top, total, acc)


def per_device(
    hidden_in,
    ffn_gain,
    wi_gate,
    wi_up,
    wo_down,
    final_gain,
    key_w,
    value_w,
    query_w,
    out_w,
    dec_gain,
    embed,
    lengths,
    answer_ids,
):
    rows = hidden_in.shape[0]
    resid_in = hidden_in.astype(jnp.float32)
    enc_in = rms_scale(resid_in, ffn_gain).astype(jnp.bfloat16)
    gate_full, up_full = in_one_piece((wi_gate, wi_up), WIDE, 0, 1)
    gate = jnp.dot(enc_in, gate_full, preferred_element_type=jnp.float32)
    up = jnp.dot(enc_in, up_full, preferred_element_type=jnp.float32)
    inner = (jax.nn.gelu(gate, approximate=True) * up).astype(jnp.bfloat16)
    down_full = whole_of(wo_down, WIDE, (0, 1), 1)
    partial_down = jnp.dot(inner, down_full, preferred_element_type=jnp.float32)
    resid = resid_in + over_copies(partial_down, "narrow")
    memory = rms_scale(resid, final_gain).astype(jnp.bfloat16)
    pass_dev = lengths.shape[0]
    per_question = pass_dev * lax.axis_size(WIDE) // QUEST
    question = lax.axis_index(WIDE) * pass_dev // per_question
    answers = answer_ids.shape[1]
    qrows = answer_ids.shape[0] * answers
    vocab_rows = embed.shape[0]
    local_ids = answer_ids.reshape(qrows) - lax.axis_index(WIDE) * vocab_rows
    onehot = (local_ids[:, None] == jnp.arange(vocab_rows, dtype=jnp.int32)[None, :]).astype(
        jnp.bfloat16
    )
    embedded = lax.psum(jnp.dot(onehot, embed, preferred_element_type=jnp.float32), WIDE)
    dec_in = rms_scale(embedded, dec_gain).astype(jnp.bfloat16)
    own_rows = lax.dynamic_slice_in_dim(dec_in, question * answers, answers, 0)
    proj_cols = key_w.shape[1]
    key_full, value_full, query_full = in_one_piece((key_w, value_w, query_w), WIDE, 0, 1)
    keys_sum = jnp.dot(memory, key_full, preferred_element_type=jnp.float32)
    values_sum = jnp.dot(memory, value_full, preferred_element_type=jnp.float32)
    query_sum = jnp.dot(own_rows, query_full, preferred_element_type=jnp.float32)
    keys = keys_sum.astype(jnp.bfloat16)
    values = values_sum.astype(jnp.bfloat16)
    query = query_sum.astype(jnp.bfloat16)
    heads_local = proj_cols // HEAD_DIM
    query_three = query.reshape(answers, heads_local, HEAD_DIM)
    keys_three = keys.reshape(rows, heads_local, HEAD_DIM)
    values_three = values.reshape(rows, heads_local, HEAD_DIM).astype(jnp.float32)
    scores = jnp.einsum(
        "ahd,khd->ahk", query_three, keys_three, preferred_element_type=jnp.float32
    ) * (1.0 / math.sqrt(HEAD_DIM))
    passage_len = rows // pass_dev
    live = (jnp.arange(passage_len, dtype=jnp.int32)[None, :] < lengths[:, None]).reshape(rows)
    scores = jnp.where(live[None, None, :], scores, FLOOR)
    top = jnp.max(scores, axis=2)
    weights = jnp.exp(scores - top[:, :, None])
    total = jnp.sum(weights, axis=2)
    acc = jnp.einsum("ahk,khd->ahd", weights, values_three).reshape(answers, proj_cols)
    start_row = question * answers
    top_all = lax.dynamic_update_slice_in_dim(
        jnp.full((qrows, heads_local), FLOOR, jnp.float32), top, start_row, 0
    )
    total_all = lax.dynamic_update_slice_in_dim(
        jnp.zeros((qrows, heads_local), jnp.float32), total, start_row, 0
    )
    acc_all = lax.dynamic_update_slice_in_dim(
        jnp.zeros((qrows, proj_cols), jnp.float32), acc, start_row, 0
    )
    top_all, total_all, acc_all = joined_all((top_all, total_all, acc_all), WIDE, join_partial)
    attended = (acc_all / jnp.repeat(total_all, HEAD_DIM, axis=1)).astype(jnp.bfloat16)
    out_full = whole_of(out_w, WIDE, (0, 1), 1)
    partial_out = jnp.dot(attended, out_full, preferred_element_type=jnp.float32)
    share_out = sum_at_owner(partial_out.astype(jnp.bfloat16), "narrow", 1)
    out_half = share_out.shape[1]
    embedded_half = lax.dynamic_slice_in_dim(
        embedded, lax.axis_index("narrow") * out_half, out_half, 1
    )
    decoded = (embedded_half + share_out).astype(jnp.bfloat16)
    return (memory, decoded)


def solution(mesh):
    torus = Mesh(
        mesh.devices.reshape(mesh.shape["groups"], 8, 16, mesh.shape["narrow"]),
        ("groups", "wide_0", "wide_1", "narrow"),
    )
    return jax.shard_map(
        per_device,
        mesh=torus,
        in_specs=(
            P(GROUPS_WIDE, None),
            P(),
            P(WIDE, "narrow"),
            P(WIDE, "narrow"),
            P("narrow", WIDE),
            P(),
            P(WIDE, "narrow"),
            P(WIDE, "narrow"),
            P(WIDE, "narrow"),
            P("narrow", WIDE),
            P(),
            P(WIDE, None),
            P(GROUPS_WIDE),
            P("groups", None),
        ),
        out_specs=(P(GROUPS_WIDE, None), P("groups", "narrow")),
        check_vma=False,
    )
```

profile of v0, /device:TPU:65, one launch (start us, length us, event | category | flops | bytes accessed | tf_op | source)
XLA Modules:
  0.0 730.1 jit_solution(12528337579370721748)
XLA Ops:
  9.1 1.1 fusion.40
  10.3 23.2 %all-gather = bf16[11264,8]{0,1:T(8,128)(2,1)} all-gather(bf16[1408,8]{0,1:T(8,128)(2,1)} %param.18), channel_id=2, replica_groups=mesh['groups'=2,'wide_0'=8,'wide_1'=16,'narrow'=2] {'wide_0'}, dimensions={0}, use_global_device_ids=true | all-gather | bytes 202752 | tf_op jit(solution)/shard_map/all_gather | solution.py:34
  33.6 1.3 pad_maximum_fusion.1
  35.1 1.4 pad_maximum_fusion
  38.4 277.3 %all-reduce.2.cloned.1.call-done = f32[128,1024]{1,0:T(8,128)} async-done(((f32[128,1024]{1,0:T(8,128)}), f32[128,1024]{1,0:T(8,128)}) %all-reduce.2.cloned.1.call-update) | async-done | bytes 524304 | tf_op jit(solution)/shard_map/psum | solution.py:148
  315.7 1.2 multiply_reduce_fusion.1
  317.0 3.8 copy.413
  320.8 1.5 convolution_convert_fusion.3
  323.1 111.4 %all-gather.15.cloned.1.call-done = bf16[1024,2816]{1,0:T(8,128)(2,1)} async-done(((bf16[8,2816]{1,0:T(8,128)(2,1)}), bf16[1024,2816]{1,0:T(8,128)(2,1)}) %all-gather.15.cloned.1.call-update) | async-done | bytes 5767184 | tf_op jit(solution)/shard_map/all_gather | solution.py:22
  434.4 4.9 fusion.12
  439.4 6.1 fusion.24
  445.9 15.5 %all_to_all.10 = f32[2,400,1024]{2,1,0:T(8,128)} all-to-all(f32[2,400,1024]{2,1,0:T(8,128)S(1)} %broadcast_in_dim.170), channel_id=1, replica_groups=mesh['groups'=2,'wide_0'=8,'wide_1'=16,'narrow'=2] {'narrow'}, dimensions={0} | all-to-all | bytes 6553600 | tf_op jit(solution)/shard_map/all_to_all | solution.py:47
  461.4 2.4 reduce_sum.55
  464.4 0.9 copy-done.3
  465.3 1.8 convolution_convert_fusion
  468.3 1.8 convolution_convert_fusion.1
  471.7 21.1 %all-gather.4 = bf16[4096,8]{0,1:T(8,128)(2,1)} all-gather(bf16[512,8]{0,1:T(8,128)(2,1)S(1)} %copy-done.8), channel_id=6, replica_groups=mesh['groups'=2,'wide_0'=8,'wide_1'=16,'narrow'=2] {'wide_0'}, dimensions={0}, use_global_device_ids=true | all-gather | bytes 73728 | tf_op jit(solution)/shard_map/all_gather | solution.py:34
  493.2 16.7 %all-gather.23.cloned.1.call-done = f32[8,132,512]{2,1,0:T(8,128)} async-done(((f32[1,132,512]{2,1,0:T(8,128)}), f32[8,132,512]{2,1,0:T(8,128)}) %all-gather.23.cloned.1.call-update) | async-done | bytes 2162704 | tf_op jit(solution)/shard_map/all_gather | solution.py:62
  509.8 1.0 fusion.51
  511.2 2.6 fusion.96
  514.4 1.1 copy.515
  515.5 1.8 copy.514
  517.3 0.8 copy.513
  518.1 0.8 fusion.95
  520.4 1.2 fusion.27
  521.7 0.9 copy.446
  522.7 54.6 %all-gather.21.cloned.1.call-done = bf16[128,512,8]{1,2,0:T(8,128)(2,1)} async-done(((bf16[8,512,8]{1,2,0:T(8,128)(2,1)}), bf16[128,512,8]{1,2,0:T(8,128)(2,1)}) %all-gather.21.cloned.1.call-update) | async-done | bytes 1048592 | tf_op jit(solution)/shard_map/all_gather | solution.py:34
  577.2 1.3 copy.511
  578.6 79.3 %all-gather.25.cloned.1.call-done = f32[16,132,512]{2,1,0:T(8,128)} async-done(((f32[1,132,512]{2,1,0:T(8,128)}), f32[16,132,512]{2,1,0:T(8,128)}) %all-gather.25.cloned.1.call-update) | async-done | bytes 4325392 | tf_op jit(solution)/shard_map/all_gather | solution.py:62
  657.8 3.8 fusion.94
  662.2 1.1 copy.532
  663.3 1.8 copy.531
  665.1 1.8 copy.530
  666.9 1.8 copy.529
  668.7 1.8 copy.528
  670.5 1.8 copy.527
  672.3 1.8 copy.526
  674.1 1.8 copy.525
  675.8 1.8 copy.524
  677.6 1.8 copy.523
  679.4 1.8 copy.522
  681.2 1.8 copy.521
  683.0 1.5 fusion.93
  685.5 1.6 fusion.92
  699.5 0.8 squeeze.274
  705.2 1.0 multiply_add_fusion
  706.2 2.6 divide_convert_fusion
  709.3 12.7 %all_to_all.11 = bf16[2,128,512]{2,1,0:T(8,128)(2,1)S(1)} all-to-all(bf16[2,128,512]{2,1,0:T(8,128)(2,1)S(1)} %bitcast.360), channel_id=1, replica_groups=mesh['groups'=2,'wide_0'=8,'wide_1'=16,'narrow'=2] {'narrow'}, dimensions={0} | all-to-all | bytes 524288 | tf_op jit(solution)/shard_map/all_to_all | solution.py:88
  (170 shorter events, 30.3 us)
Async XLA Ops:
  8.0 1.0 copy-start
  8.1 30.0 %copy-start.9 = (bf16[1024]{0:T(1024)(128)(2,1)S(1)}, bf16[1024]{0:T(1024)(128)(2,1)}, u32[]{:S(2)}) copy-start(bf16[1024]{0:T(1024)(128)(2,1)} %param.24) | copy-start | bytes 6148
  8.1 30.0 %copy-start.10 = (s32[2]{0:T(128)S(1)}, s32[2]{0:T(128)}, u32[]{:S(2)}) copy-start(s32[2]{0:T(128)} %param.26) | copy-start | bytes 28
  8.1 30.1 %copy-start.1 = (bf16[400,1024]{1,0:T(8,128)(2,1)S(1)}, bf16[400,1024]{1,0:T(8,128)(2,1)}, u32[]{:S(2)}) copy-start(bf16[400,1024]{1,0:T(8,128)(2,1)} %param.14) | copy-start | bytes 2457604
  8.1 307.7 %all-reduce.2.cloned.1.call-start = ((), (), s32[]{:S(2)}) async-start(), calls=%async_computation.3 | async-start | bytes 1048576 | tf_op jit(solution)/shard_map/psum | solution.py:148
  10.2 306.8 %all-gather.19.cloned.1.call-start = ((), (), s32[]{:S(2)}) async-start(), calls=%async_computation.5 | async-start | bytes 3063808 | tf_op jit(solution)/shard_map/all_gather | solution.py:34
  33.6 287.2 %all-gather.17.cloned.1.call-start = ((), (), s32[]{:S(2)}) async-start(), calls=%async_computation.4 | async-start | bytes 3170304 | tf_op jit(solution)/shard_map/all_gather | solution.py:22
  35.0 399.4 %all-gather.15.cloned.1.call-start = ((), (), s32[]{:S(2)}) async-start(), calls=%async_computation.2 | async-start | bytes 5812224 | tf_op jit(solution)/shard_map/all_gather | solution.py:22
  36.6 473.3 %all-gather.23.cloned.1.call-start = ((), (), s32[]{:S(2)}) async-start(), calls=%async_computation.7 | async-start | bytes 2506752 | tf_op jit(solution)/shard_map/all_gather | solution.py:62
  317.0 3.8 copy-start.2
  464.4 0.9 copy-start.3
  465.2 2.1 copy-start.5
  467.1 1.1 copy-start.4
  470.1 1.6 copy-start.8
  471.6 105.6 %all-gather.21.cloned.1.call-start = ((), (), s32[]{:S(2)}) async-start(), calls=%async_computation.6 | async-start | bytes 1114112 | tf_op jit(solution)/shard_map/all_gather | solution.py:34
  492.9 164.9 %all-gather.25.cloned.1.call-start = ((), (), s32[]{:S(2)}) async-start(), calls=%async_computation.8 | async-start | bytes 4734976 | tf_op jit(solution)/shard_map/all_gather | solution.py:62
  691.4 10.7 %copy-start.6 = (f32[1,2,512]{2,1,0:T(2,128)S(1)}, f32[1,2,512]{2,1,0:T(2,128)}, u32[]{:S(2)}) copy-start(f32[1,2,512]{2,1,0:T(2,128)} %get-tuple-element.67) | copy-start | bytes 12292
  692.2 9.8 %copy-start.7 = (f32[1,2,512]{2,1,0:T(2,128)S(1)}, f32[1,2,512]{2,1,0:T(2,128)}, u32[]{:S(2)}) copy-start(f32[1,2,512]{2,1,0:T(2,128)} %get-tuple-element.76) | copy-start | bytes 12292
Sparse Core Ops, SparseCore 0:
  13.0 302.6 all-reduce.1
  471.8 38.0 all-gather.22
  511.9 65.2 all-gather.20
  579.2 78.5 all-gather.24
Sparse Core Ops, SparseCore 1:
  33.7 106.3 all-gather.18
  143.5 142.1 all-gather.16
  288.5 145.9 all-gather.14
where the time goes:
time: 732 us; the launch traced here: 730 us
  waiting for transfers between devices  540 us (74%)
  blocking collectives  72.5 us (10%)
  local copies, waits for them, and re-layouts  65.7 us (9%)
  matrix products  18.4 us (3%)
  other arithmetic  17 us (2%)
  between operations  16.3 us (2%)
    psum x1, waiting for transfers between devices, per_device(): lax.psum(jnp.dot(onehot, embed, preferred_element_type=jnp.float32), WIDE)  277 us
    all_gather x2, waiting for transfers between devices, in_one_piece(): lax.all_gather(both, axis, axis=dim, tiled=True)  111 us
    all_gather x2, waiting for transfers between devices, collected_together(): both, at, found = (lax.all_gather(jnp.concatenate(lines), axis), 0, {})  95.9 us
    all_gather x2, waiting for transfers between devices, all_blocks(): tiles = lax.all_gather(tiles, axes[k])  54.6 us
    all_gather x2, blocking collectives, all_blocks(): tiles = lax.all_gather(tiles, axes[k])  44.4 us
    unnamed x47, local copies, waits for them, and re-layouts  27.5 us
    squeeze x74, local copies, waits for them, and re-layouts, joined_all(): x = combine(x, jax.tree.map(lambda part: part[k], pieces))  18.4 us
    all_to_all x1, blocking collectives, from_everyone(): return lax.all_to_all(copies, axis, split_axis=0, concat_axis=0, tiled=True)  15.5 us
  transfers between devices with their start and end apart: 7, of which 5 were waited for; matrix products, arithmetic and copies ran while one was open for 4% of the time, Pallas kernels for 0%

commit v1 on v0

--- a/solution.py
+++ b/solution.py
@@ -145,7 +145,8 @@
     onehot = (local_ids[:, None] == jnp.arange(vocab_rows, dtype=jnp.int32)[None, :]).astype(
         jnp.bfloat16
     )
-    embedded = lax.psum(jnp.dot(onehot, embed, preferred_element_type=jnp.float32), WIDE)
+    partial = lax.psum(jnp.dot(onehot, embed, preferred_element_type=jnp.float32), "wide_0")
+    embedded = lax.psum(partial, "wide_1")
     dec_in = rms_scale(embedded, dec_gain).astype(jnp.bfloat16)
     own_rows = lax.dynamic_slice_in_dim(dec_in, question * answers, answers, 0)
     proj_cols = key_w.shape[1]

time: 732 us -> 932 us (1.27)
  waiting for transfers between devices: 540 us -> 746 us
    all_gather x2, waiting for transfers between devices: 111 us -> 288 us  [in_one_piece(): lax.all_gather(both, axis, axis=dim, tiled=True)]
    all_gather x2, waiting for transfers between devices: 54.6 us -> 129 us  [all_blocks(): tiles = lax.all_gather(tiles, axes[k])]
    psum x1 -> x2, waiting for transfers between devices: 277 us -> 233 us  [the longest x1 118 us: per_device(): lax.psum(jnp.dot(onehot, embed, preferred_element_type=jnp.float32), 'wid...]
    unnamed x47 -> x61, local copies, waits for them, and re-layouts: 27.5 us -> 27.4 us
  transfers between devices with their start and end apart: 7 -> 8, of which waited for: 5 -> 8; matrix products, arithmetic and copies ran while one was open for 4% -> 2% of each run, Pallas kernels for 0% -> 0%
where the time goes in v1:
time: 932 us; the launch traced here: 931 us
  waiting for transfers between devices  746 us (80%)
  blocking collectives  70.7 us (8%)
  local copies, waits for them, and re-layouts  65.5 us (7%)
  matrix products  18.4 us (2%)
  between operations  15.1 us (2%)
  other arithmetic  14.3 us (2%)
    all_gather x2, waiting for transfers between devices, in_one_piece(): lax.all_gather(both, axis, axis=dim, tiled=True)  288 us
    all_gather x2, waiting for transfers between devices, all_blocks(): tiles = lax.all_gather(tiles, axes[k])  129 us
    psum x1, waiting for transfers between devices, per_device(): lax.psum(jnp.dot(onehot, embed, preferred_element_type=jnp.float32), 'wid...  118 us
    psum x1, waiting for transfers between devices, per_device(): embedded = lax.psum(partial, 'wide_1')  115 us
    all_gather x2, waiting for transfers between devices, collected_together(): both, at, found = (lax.all_gather(jnp.concatenate(lines), axis), 0, {})  95.5 us
    all_gather x2, blocking collectives, all_blocks(): tiles = lax.all_gather(tiles, axes[k])  42.2 us
    unnamed x61, local copies, waits for them, and re-layouts  27.4 us
  transfers between devices with their start and end apart: 8, of which 8 were waited for; matrix products, arithmetic and copies ran while one was open for 2% of the time, Pallas kernels for 0%

profile of v1, /device:TPU:65, one launch (start us, length us, event | category | flops | bytes accessed | tf_op | source)
XLA Modules:
  0.0 930.8 jit_solution(6448531791263369525)
XLA Ops:
  7.4 0.9 broadcast_subtract_fusion
  8.3 1.1 fusion.40
  9.5 117.7 %all-reduce.3.cloned.1.call-done = f32[128,1024]{1,0:T(8,128)} async-done(((f32[128,1024]{1,0:T(8,128)}), f32[128,1024]{1,0:T(8,128)}) %all-reduce.3.cloned.1.call-update) | async-done | bytes 524304 | tf_op jit(solution)/shard_map/psum | solution.py:148
  127.4 21.0 %all-gather = bf16[11264,8]{0,1:T(8,128)(2,1)} all-gather(bf16[1408,8]{0,1:T(8,128)(2,1)} %param.18), channel_id=2, replica_groups=mesh['groups'=2,'wide_0'=8,'wide_1'=16,'narrow'=2] {'wide_0'}, dimensions={0}, use_global_device_ids=true | all-gather | bytes 202752 | tf_op jit(solution)/shard_map/all_gather | solution.py:34
  150.6 114.9 %all-reduce.5.cloned.1.call-done = f32[128,1024]{1,0:T(8,128)} async-done(((f32[128,1024]{1,0:T(8,128)}), f32[128,1024]{1,0:T(8,128)}) %all-reduce.5.cloned.1.call-update) | async-done | bytes 524304 | tf_op jit(solution)/shard_map/psum | solution.py:149
  265.4 1.2 multiply_reduce_fusion.1
  266.7 74.6 %all-gather.19.cloned.1.call-done = bf16[128,1408,8]{1,2,0:T(8,128)(2,1)} async-done(((bf16[8,1408,8]{1,2,0:T(8,128)(2,1)}), bf16[128,1408,8]{1,2,0:T(8,128)(2,1)}) %all-gather.19.cloned.1.call-update) | async-done | bytes 2883600 | tf_op jit(solution)/shard_map/all_gather | solution.py:34
  341.3 3.7 copy.413
  345.0 141.3 %all-gather.17.cloned.1.call-done = bf16[1024,1536]{1,0:T(8,128)(2,1)} async-done(((bf16[8,1536]{1,0:T(8,128)(2,1)}), bf16[1024,1536]{1,0:T(8,128)(2,1)}) %all-gather.17.cloned.1.call-update) | async-done | bytes 3145744 | tf_op jit(solution)/shard_map/all_gather | solution.py:22
  486.3 1.5 convolution_convert_fusion.3
  488.6 147.0 %all-gather.15.cloned.1.call-done = bf16[1024,2816]{1,0:T(8,128)(2,1)} async-done(((bf16[8,2816]{1,0:T(8,128)(2,1)}), bf16[1024,2816]{1,0:T(8,128)(2,1)}) %all-gather.15.cloned.1.call-update) | async-done | bytes 5767184 | tf_op jit(solution)/shard_map/all_gather | solution.py:22
  635.6 4.9 fusion.12
  640.6 6.1 fusion.24
  647.1 15.8 %all_to_all.10 = f32[2,400,1024]{2,1,0:T(8,128)} all-to-all(f32[2,400,1024]{2,1,0:T(8,128)S(1)} %broadcast_in_dim.170), channel_id=1, replica_groups=mesh['groups'=2,'wide_0'=8,'wide_1'=16,'narrow'=2] {'narrow'}, dimensions={0} | all-to-all | bytes 6553600 | tf_op jit(solution)/shard_map/all_to_all | solution.py:47
  662.9 2.4 reduce_sum.55
  665.9 0.9 copy-done.3
  666.8 1.9 convolution_convert_fusion
  669.8 1.8 convolution_convert_fusion.1
  673.3 21.2 %all-gather.4 = bf16[4096,8]{0,1:T(8,128)(2,1)} all-gather(bf16[512,8]{0,1:T(8,128)(2,1)S(1)} %copy-done.10), channel_id=6, replica_groups=mesh['groups'=2,'wide_0'=8,'wide_1'=16,'narrow'=2] {'wide_0'}, dimensions={0}, use_global_device_ids=true | all-gather | bytes 73728 | tf_op jit(solution)/shard_map/all_gather | solution.py:34
  694.8 16.1 %all-gather.23.cloned.1.call-done = f32[8,132,512]{2,1,0:T(8,128)} async-done(((f32[1,132,512]{2,1,0:T(8,128)}), f32[8,132,512]{2,1,0:T(8,128)}) %all-gather.23.cloned.1.call-update) | async-done | bytes 2162704 | tf_op jit(solution)/shard_map/all_gather | solution.py:62
  710.9 1.0 fusion.51
  712.2 2.6 fusion.96
  715.4 1.1 copy.515
  716.5 1.8 copy.514
  719.2 0.8 fusion.95
  721.4 1.2 fusion.27
  722.8 0.9 copy.446
  723.8 54.7 %all-gather.21.cloned.1.call-done = bf16[128,512,8]{1,2,0:T(8,128)(2,1)} async-done(((bf16[8,512,8]{1,2,0:T(8,128)(2,1)}), bf16[128,512,8]{1,2,0:T(8,128)(2,1)}) %all-gather.21.cloned.1.call-update) | async-done | bytes 1048592 | tf_op jit(solution)/shard_map/all_gather | solution.py:34
  778.4 1.3 copy.511
  779.8 79.4 %all-gather.25.cloned.1.call-done = f32[16,132,512]{2,1,0:T(8,128)} async-done(((f32[1,132,512]{2,1,0:T(8,128)}), f32[16,132,512]{2,1,0:T(8,128)}) %all-gather.25.cloned.1.call-update) | async-done | bytes 4325392 | tf_op jit(solution)/shard_map/all_gather | solution.py:62
  859.2 3.8 fusion.94
  863.5 1.1 copy.532
  864.6 1.8 copy.531
  866.4 1.8 copy.530
  868.2 1.8 copy.529
  870.0 1.8 copy.528
  871.8 1.8 copy.527
  873.6 1.8 copy.526
  875.3 1.8 copy.525
  877.1 1.8 copy.524
  878.9 1.8 copy.523
  880.7 1.8 copy.522
  882.5 1.8 copy.521
  884.3 1.5 fusion.93
  886.7 1.6 fusion.92
  906.5 1.0 multiply_add_fusion
  907.5 2.6 divide_convert_fusion
  910.6 12.7 %all_to_all.11 = bf16[2,128,512]{2,1,0:T(8,128)(2,1)S(1)} all-to-all(bf16[2,128,512]{2,1,0:T(8,128)(2,1)S(1)} %bitcast.360), channel_id=1, replica_groups=mesh['groups'=2,'wide_0'=8,'wide_1'=16,'narrow'=2] {'narrow'}, dimensions={0} | all-to-all | bytes 524288 | tf_op jit(solution)/shard_map/all_to_all | solution.py:88
  (187 shorter events, 31.1 us)
Async XLA Ops:
  7.2 1.2 copy-start
  7.2 141.3 %copy-start.11 = (bf16[8,512]{1,0:T(8,128)(2,1)S(1)}, bf16[8,512]{1,0:T(8,128)(2,1)}, u32[]{:S(2)}) copy-start(bf16[8,512]{1,0:T(8,128)(2,1)} %param.22) | copy-start | bytes 24580
  7.2 141.3 %copy-start.12 = (bf16[8,512]{1,0:T(8,128)(2,1)S(1)}, bf16[8,512]{1,0:T(8,128)(2,1)}, u32[]{:S(2)}) copy-start(bf16[8,512]{1,0:T(8,128)(2,1)} %param.21) | copy-start | bytes 24580
  7.2 141.3 %copy-start.13 = (bf16[8,512]{1,0:T(8,128)(2,1)S(1)}, bf16[8,512]{1,0:T(8,128)(2,1)}, u32[]{:S(2)}) copy-start(bf16[8,512]{1,0:T(8,128)(2,1)} %param.20) | copy-start | bytes 24580
  7.2 142.0 %copy-start.6 = (bf16[8,1408]{1,0:T(8,128)(2,1)S(1)}, bf16[8,1408]{1,0:T(8,128)(2,1)}, u32[]{:S(2)}) copy-start(bf16[8,1408]{1,0:T(8,128)(2,1)} %param.17) | copy-start | bytes 67588
  7.2 142.0 %copy-start.7 = (bf16[8,1408]{1,0:T(8,128)(2,1)S(1)}, bf16[8,1408]{1,0:T(8,128)(2,1)}, u32[]{:S(2)}) copy-start(bf16[8,1408]{1,0:T(8,128)(2,1)} %param.16) | copy-start | bytes 67588
  7.2 142.8 %copy-start.14 = (bf16[1024]{0:T(1024)(128)(2,1)S(1)}, bf16[1024]{0:T(1024)(128)(2,1)}, u32[]{:S(2)}) copy-start(bf16[1024]{0:T(1024)(128)(2,1)} %param.15) | copy-start | bytes 6148
  7.3 142.8 %copy-start.15 = (bf16[1024]{0:T(1024)(128)(2,1)S(1)}, bf16[1024]{0:T(1024)(128)(2,1)}, u32[]{:S(2)}) copy-start(bf16[1024]{0:T(1024)(128)(2,1)} %param.19) | copy-start | bytes 6148
  7.3 142.9 %copy-start.16 = (bf16[1024]{0:T(1024)(128)(2,1)S(1)}, bf16[1024]{0:T(1024)(128)(2,1)}, u32[]{:S(2)}) copy-start(bf16[1024]{0:T(1024)(128)(2,1)} %param.24) | copy-start | bytes 6148
  7.3 142.9 %copy-start.17 = (s32[2]{0:T(128)S(1)}, s32[2]{0:T(128)}, u32[]{:S(2)}) copy-start(s32[2]{0:T(128)} %param.26) | copy-start | bytes 28
  7.3 143.0 %copy-start.1 = (bf16[400,1024]{1,0:T(8,128)(2,1)S(1)}, bf16[400,1024]{1,0:T(8,128)(2,1)}, u32[]{:S(2)}) copy-start(bf16[400,1024]{1,0:T(8,128)(2,1)} %param.14) | copy-start | bytes 2457604
  7.3 120.0 %all-reduce.3.cloned.1.call-start = ((), (), s32[]{:S(2)}) async-start(), calls=%async_computation.3 | async-start | bytes 1048576 | tf_op jit(solution)/shard_map/psum | solution.py:148
  9.5 256.0 %all-reduce.5.cloned.1.call-start = ((), (), s32[]{:S(2)}) async-start(), calls=%async_computation.4 | async-start | bytes 1048576 | tf_op jit(solution)/shard_map/psum | solution.py:149
  127.3 214.0 %all-gather.19.cloned.1.call-start = ((), (), s32[]{:S(2)}) async-start(), calls=%async_computation.6 | async-start | bytes 3063808 | tf_op jit(solution)/shard_map/all_gather | solution.py:34
  148.4 337.9 %all-gather.17.cloned.1.call-start = ((), (), s32[]{:S(2)}) async-start(), calls=%async_computation.5 | async-start | bytes 3170304 | tf_op jit(solution)/shard_map/all_gather | solution.py:22
  149.2 486.4 %all-gather.15.cloned.1.call-start = ((), (), s32[]{:S(2)}) async-start(), calls=%async_computation.2 | async-start | bytes 5812224 | tf_op jit(solution)/shard_map/all_gather | solution.py:22
  150.0 560.9 %all-gather.23.cloned.1.call-start = ((), (), s32[]{:S(2)}) async-start(), calls=%async_computation.8 | async-start | bytes 2506752 | tf_op jit(solution)/shard_map/all_gather | solution.py:62
  341.3 145.0 %copy-start.2 = (f32[128,1024]{1,0:T(8,128)S(1)}, f32[128,1024]{1,0:T(8,128)}, u32[]{:S(2)}) copy-start(f32[128,1024]{1,0:T(8,128)} %all-reduce.5.cloned.1.call-done) | copy-start | bytes 1572868
  665.9 0.9 copy-start.3
  666.8 2.1 copy-start.5
  668.6 1.1 copy-start.4
  671.6 1.6 copy-start.10
  673.2 105.3 %all-gather.21.cloned.1.call-start = ((), (), s32[]{:S(2)}) async-start(), calls=%async_computation.7 | async-start | bytes 1114112 | tf_op jit(solution)/shard_map/all_gather | solution.py:34
  694.5 164.6 %all-gather.25.cloned.1.call-start = ((), (), s32[]{:S(2)}) async-start(), calls=%async_computation.9 | async-start | bytes 4734976 | tf_op jit(solution)/shard_map/all_gather | solution.py:62
  892.7 10.7 %copy-start.8 = (f32[1,2,512]{2,1,0:T(2,128)S(1)}, f32[1,2,512]{2,1,0:T(2,128)}, u32[]{:S(2)}) copy-start(f32[1,2,512]{2,1,0:T(2,128)} %get-tuple-element.67) | copy-start | bytes 12292
  893.5 9.8 %copy-start.9 = (f32[1,2,512]{2,1,0:T(2,128)S(1)}, f32[1,2,512]{2,1,0:T(2,128)}, u32[]{:S(2)}) copy-start(f32[1,2,512]{2,1,0:T(2,128)} %get-tuple-element.76) | copy-start | bytes 12292
Sparse Core Ops, SparseCore 0:
  11.1 116.1 all-reduce.2
  129.6 135.7 all-reduce.4
  267.5 73.7 all-gather.18
  344.7 141.5 all-gather.16
  489.7 145.8 all-gather.14
  673.3 37.5 all-gather.22
  713.0 65.3 all-gather.20
  780.5 78.5 all-gather.24
